TPU v7x, 32 devices: a whole 2x2x4 slice. The times are simulated.
32 devices in a mesh: grp: 1, blk: 8 (over z, y), node: 4 (over x, core), pair: 1.
Axes of the slice: x: 2, y: 2, z: 4, core: 2. Of those that a mesh axis runs over, the one named last changes fastest.
Arguments:
- query: bfloat16 [4608, 1280], P(('grp', 'blk', 'node'), 'pair'), may hold values from -600 to 600
- key: bfloat16 [4608, 1280], P(('grp', 'blk', 'node'), 'pair'), may hold values from -25 to 25
- value: bfloat16 [4608, 1280], P(('grp', 'blk', 'node'), 'pair'), may hold values from -6 to 6
- out_weight: bfloat16 [1280, 1280], P('pair'), may hold values from -0.15625 to 0.15625
Outputs:
- mixed: bfloat16 [4608, 1280], P(('grp', 'blk', 'node', 'pair'))
All inputs are finite; a program needn't handle non-finite values.
Results may differ from a plain program's by a relative error of at most 0.011.
Values may be sent and summed in bfloat16 or wider, within the bound.
A program may use at most 128 MiB of HBM per device.

v0:
```python
import math
import jax
import jax.numpy as jnp
from jax import lax
from jax.sharding import PartitionSpec as P

HD = 64
lowest = -1e30


def block_rows(count):
    size = count
    while size > 1024 and size % 2 == 0:
        size = size // 2
    return size


def attend(carry, keys_piece, values_piece, queries):
    count = keys_piece.shape[0]
    size = block_rows(count)
    q_rows, heads, width = queries.shape
    scale = 1.0 / math.sqrt(width)

    def update(turn, state):
        peak, total, accum = state
        key_block = lax.dynamic_slice_in_dim(keys_piece, turn * size, size, 0).reshape(
            size, heads, width
        )
        value_block = lax.dynamic_slice_in_dim(values_piece, turn * size, size, 0).reshape(
            size, heads, width
        )
        scores = (
            jnp.einsum("qhd,khd->hqk", queries, key_block, preferred_element_type=jnp.float32)
            * scale
        )
        fresh = jnp.maximum(peak, jnp.max(scores, axis=2))
        expo = jnp.exp(scores - fresh[:, :, None])
        factor = jnp.exp(peak - fresh)
        total = total * factor + jnp.sum(expo, axis=2)
        weighted = jnp.einsum(
            "hqk,khd->qhd",
            expo.astype(jnp.bfloat16),
            value_block,
            preferred_element_type=jnp.float32,
        )
        accum = (accum.reshape(q_rows, heads, width) * factor.T[:, :, None] + weighted).reshape(
            q_rows, heads * width
        )
        return (fresh, total, accum)

    return lax.fori_loop(0, count // size, update, carry)


def start_state(heads, count, features):
    return (
        jnp.full((heads, count), lowest, jnp.float32),
        jnp.zeros((heads, count), jnp.float32),
        jnp.zeros((count, features), jnp.float32),
    )


def per_device(query, key, value, out_weight):
    rows, features = query.shape
    heads = features // HD
    gathered = lax.all_gather(query, "node", axis=0, tiled=True)
    count = gathered.shape[0]
    q_three = gathered.reshape(count, heads, HD)
    peak, total, accum = attend(
        start_state(heads, count, features),
        lax.all_gather(key, "blk", axis=0, tiled=True),
        lax.all_gather(value, "blk", axis=0, tiled=True),
        q_three,
    )
    nodes = lax.axis_size("node")
    acc_parts = accum.reshape(nodes, rows, features)
    peak_parts = peak.T.reshape(nodes, rows, heads)
    total_parts = total.T.reshape(nodes, rows, heads)
    acc_in = lax.all_to_all(acc_parts, "node", split_axis=0, concat_axis=0, tiled=True)
    peak_in = lax.all_to_all(peak_parts, "node", split_axis=0, concat_axis=0, tiled=True)
    total_in = lax.all_to_all(total_parts, "node", split_axis=0, concat_axis=0, tiled=True)
    sources = acc_in.shape[0]
    items = acc_in.shape[1]
    best = jnp.max(peak_in, axis=0)
    weight = jnp.exp(peak_in - best[None])
    summed = jnp.sum(weight * total_in, axis=0)
    joined = jnp.sum(acc_in.reshape(sources, items, heads, HD) * weight[:, :, :, None], axis=0)
    attn = (joined / summed[:, :, None]).reshape(items, features).astype(jnp.bfloat16)
    return lax.psum_scatter(
        jnp.dot(attn, out_weight, preferred_element_type=jnp.float32).astype(jnp.bfloat16),
        "pair",
        scatter_dimension=0,
        tiled=True,
    )


def solution(mesh):
    in_specs = (
        P(("grp", "blk", "node"), "pair"),
        P(("grp", "blk", "node"), "pair"),
        P(("grp", "blk", "node"), "pair"),
        P("pair", None),
    )
    out_specs = P(("grp", "blk", "node", "pair"), None)
    return jax.shard_map(
        per_device, mesh=mesh, in_specs=in_specs, out_specs=out_specs, check_vma=False
    )
```

profile of v0, /device:TPU:0, one launch (start us, length us, event | category | flops | bytes accessed | tf_op | source)
XLA Modules:
  0.0 324.1 jit_solution(2416669906681257392)
XLA Ops:
  6.5 0.7 all-gather.6.cloned.1.call-update
  7.3 0.0 all-gather.4.cloned.1.call-start
  7.3 0.7 all-gather.4.cloned.1.call-update
  8.0 0.0 all-gather.8.cloned.1.call-start
  8.1 0.7 all-gather.8.cloned.1.call-update
  8.8 22.0 %all-gather.6.cloned.1.call-done = bf16[576,1280]{1,0:T(8,128)(2,1)} async-done(((bf16[144,1280]{1,0:T(8,128)(2,1)}), bf16[576,1280]{1,0:T(8,128)(2,1)}) %all-gather.6.cloned.1.call-update) | async-done | bytes 1474576 | tf_op jit(solution)/shard_map/all_gather | solution.py:65
  30.7 2.7 copy.30
  33.4 57.5 %all-gather.4.cloned.1.call-done = bf16[1152,1280]{1,0:T(8,128)(2,1)} async-done(((bf16[144,1280]{1,0:T(8,128)(2,1)}), bf16[1152,1280]{1,0:T(8,128)(2,1)}) %all-gather.4.cloned.1.call-update) | async-done | bytes 2949136 | tf_op jit(solution)/shard_map/all_gather | solution.py:70
  90.9 58.8 %all-gather.8.cloned.1.call-done = bf16[1152,1280]{1,0:T(8,128)(2,1)} async-done(((bf16[144,1280]{1,0:T(8,128)(2,1)}), bf16[1152,1280]{1,0:T(8,128)(2,1)}) %all-gather.8.cloned.1.call-update) | async-done | bytes 2949136 | tf_op jit(solution)/shard_map/all_gather | solution.py:71
  149.7 1.9 broadcast_in_dim.20
  151.6 106.3 %while.18 = (s32[]{:T(128)}, f32[20,576]{1,0:T(8,128)S(1)}, f32[20,576]{1,0:T(8,128)}, f32[576,1280]{0,1:T(8,128)}, bf16[1152,1280]{1,0:T(8,128)(2,1)}, /*index=...) while((s32[]{:T(128)}, f32[20,576]{1,0:T(8,128)S(1)}, ...), condition=%wide.region_3.0_spmd.clone, body=%wide.region_0.0_spmd.clone.sunk | while | flops 1753320960 | bytes 102850792 | solution.py:51
  151.6 3.7 %constant_dynamic-slice_fusion.3 = (bf16[576,1280]{1,0:T(8,128)(2,1)}, bf16[576,1280]{1,0:T(8,128)(2,1)}) fusion(bf16[1152,1280]{1,0:T(8,128)(2,1)} %get-tuple-element.277, s32[]{:T(128)S(6)} %select_n.10, bf16[1152,1280]{1,0:T(8,128)(2,1)} %get-tuple-element.275), kind=kLoop, calls=%fused_computation.14.clone.1 | loop fusion | bytes 5898244 | tf_op jit(solution)/shard_map/while/body/eval_jaxpr/dynamic_slice | solution.py:29
  155.2 2.7 copy.49
  157.9 15.7 %bitcast_reduce_fusion.3 = (f32[20,576]{1,0:T(8,128)S(1)}, f32[20,576,576]{2,1,0:T(8,128)}) fusion(bf16[576,20,64]{0,2,1:T(8,128)(2,1)} %bitcast.67, bf16[576,20,64]{0,2,1:T(8,128)(2,1)} %get-tuple-element.276), kind=kOutput, calls=%fused_computation.1.clone.1 | convolution fusion | flops 862606080 | bytes 29537280 | tf_op jit(solution)/shard_map/while/body/eval_jaxpr/qhd,khd->hqk/dot_general | solution.py:33
  173.6 10.4 %fusion.28 = f32[20,576]{1,0:T(8,128)S(1)} fusion(f32[20,576,576]{2,1,0:T(8,128)} %get-tuple-element.246, f32[20,576]{1,0:T(8,128)S(1)} %get-tuple-element.272), kind=kLoop, calls=%fused_computation.4.clone.1 | loop fusion | flops 19895040 | bytes 26634240 | tf_op jit(solution)/shard_map/while/body/eval_jaxpr/reduce_sum | solution.py:39
  184.1 2.7 copy.50
  186.7 18.0 %bitcast_add_fusion.2 = f32[576,20,64]{0,2,1:T(8,128)} fusion(f32[576,20,64]{0,2,1:T(8,128)} %bitcast.70, bf16[576,20,64]{0,2,1:T(8,128)(2,1)} %bitcast.69, f32[20,576,576]{2,1,0:T(8,128)} %get-tuple-element.246, f32[20,576]{1,0:T(8,128)S(1)} %get-tuple-element.272, f32[576,20]{0,1:T(8,128)S(1)} %get-tuple-element.248), kind=kOutput, calls=%fused_computation.8.clone.1 | convolution fusion | flops 870727680 | bytes 34007040 | tf_op jit(solution)/shard_map/while/body/eval_jaxpr/hqk,khd->qhd/dot_general | solution.py:40
  204.7 3.7 %constant_dynamic-slice_fusion.3 = (bf16[576,1280]{1,0:T(8,128)(2,1)}, bf16[576,1280]{1,0:T(8,128)(2,1)}) fusion(bf16[1152,1280]{1,0:T(8,128)(2,1)} %get-tuple-element.277, s32[]{:T(128)S(6)} %select_n.10, bf16[1152,1280]{1,0:T(8,128)(2,1)} %get-tuple-element.275), kind=kLoop, calls=%fused_computation.14.clone.1 | loop fusion | bytes 5898244 | tf_op jit(solution)/shard_map/while/body/eval_jaxpr/dynamic_slice | solution.py:29
  208.4 2.7 copy.49
  211.0 15.7 %bitcast_reduce_fusion.3 = (f32[20,576]{1,0:T(8,128)S(1)}, f32[20,576,576]{2,1,0:T(8,128)}) fusion(bf16[576,20,64]{0,2,1:T(8,128)(2,1)} %bitcast.67, bf16[576,20,64]{0,2,1:T(8,128)(2,1)} %get-tuple-element.276), kind=kOutput, calls=%fused_computation.1.clone.1 | convolution fusion | flops 862606080 | bytes 29537280 | tf_op jit(solution)/shard_map/while/body/eval_jaxpr/qhd,khd->hqk/dot_general | solution.py:33
  226.7 10.4 %fusion.28 = f32[20,576]{1,0:T(8,128)S(1)} fusion(f32[20,576,576]{2,1,0:T(8,128)} %get-tuple-element.246, f32[20,576]{1,0:T(8,128)S(1)} %get-tuple-element.272), kind=kLoop, calls=%fused_computation.4.clone.1 | loop fusion | flops 19895040 | bytes 26634240 | tf_op jit(solution)/shard_map/while/body/eval_jaxpr/reduce_sum | solution.py:39
  237.2 2.7 copy.50
  239.9 18.0 %bitcast_add_fusion.2 = f32[576,20,64]{0,2,1:T(8,128)} fusion(f32[576,20,64]{0,2,1:T(8,128)} %bitcast.70, bf16[576,20,64]{0,2,1:T(8,128)(2,1)} %bitcast.69, f32[20,576,576]{2,1,0:T(8,128)} %get-tuple-element.246, f32[20,576]{1,0:T(8,128)S(1)} %get-tuple-element.272, f32[576,20]{0,1:T(8,128)S(1)} %get-tuple-element.248), kind=kOutput, calls=%fused_computation.8.clone.1 | convolution fusion | flops 870727680 | bytes 34007040 | tf_op jit(solution)/shard_map/while/body/eval_jaxpr/hqk,khd->qhd/dot_general | solution.py:40
  257.9 0.1 reshape.54
  258.0 0.7 reshape.60
  258.8 3.5 %all-to-all-start.1 = ((f32[4,1,2880]{2,1,0:T(1,128)}), f32[4,1,2880]{2,1,0:T(1,128)S(1)}, u32[]{:S(2)}, u32[]{:S(2)}) async-start(f32[4,1,2880]{2,1,0:T(1,128)} %reshape.60), calls=%async_computation.1 | async-start | bytes 94208 | tf_op jit(solution)/shard_map/all_to_all | solution.py:79
  262.2 0.9 reshape.55
  263.2 0.8 reshape.62
  263.9 2.3 all-to-all-done.1
  266.2 3.3 %all-to-all-start.2 = ((f32[4,1,2880]{2,1,0:T(1,128)}), f32[4,1,2880]{2,1,0:T(1,128)S(1)}, u32[]{:S(2)}, u32[]{:S(2)}) async-start(f32[4,1,2880]{2,1,0:T(1,128)} %reshape.62), calls=%async_computation.2 | async-start | bytes 94208 | tf_op jit(solution)/shard_map/all_to_all | solution.py:80
  269.5 3.6 %copy.33 = f32[576,1280]{1,0:T(8,128)} copy(f32[576,1280]{0,1:T(8,128)} %get-tuple-element.131) | data formatting | bytes 5898240 | tf_op jit(solution)/shard_map/while | solution.py:51
  273.0 0.4 all-to-all-done.2
  273.5 4.6 %all-to-all-start = ((f32[4,144,1280]{2,1,0:T(8,128)}), f32[4,144,1280]{2,1,0:T(8,128)}, u32[]{:S(2)}, u32[]{:S(2)}) async-start(f32[4,144,1280]{2,1,0:T(8,128)} %bitcast.72), calls=%async_computation | async-start | bytes 5898240 | tf_op jit(solution)/shard_map/all_to_all | solution.py:78
  278.1 0.5 broadcast.49
  278.6 0.8 reduce.1
  279.4 0.1 reshape.61
  279.5 0.8 reduce.2
  280.3 0.1 reshape.63
  280.4 0.7 multiply_reduce_fusion.1
  281.1 1.8 copy.35
  282.8 5.3 %mul.59 = f32[4,144,20,64]{3,2,1,0:T(8,128)} broadcast(f32[4,144,20]{2,1,0:T(8,128)} %copy.35), dimensions={0,1,2} | broadcast | bytes 2995200 | tf_op jit(solution)/shard_map/mul | solution.py:86
  288.1 6.4 %mul.60 = f32[4,144,1280]{2,1,0:T(8,128)} reshape(f32[4,144,20,64]{3,2,1,0:T(8,128)} %mul.59) | data formatting | bytes 5898240 | tf_op jit(solution)/shard_map/mul | solution.py:86
  294.5 0.1 copy.38
  294.6 1.8 div.11
  296.4 2.6 div.12
  299.0 14.0 %all-to-all-done = f32[4,144,1280]{2,1,0:T(8,128)} async-done(((f32[4,144,1280]{2,1,0:T(8,128)}), f32[4,144,1280]{2,1,0:T(8,128)}, u32[]{:S(2)}, u32[]{:S(2)}) %all-to-all-start) | async-done | bytes 2949152 | tf_op jit(solution)/shard_map/all_to_all | solution.py:78
  313.0 3.2 multiply_reduce_fusion
  316.2 1.4 convolution_convert_fusion
  (24 shorter events, 0.2 us)
Async XLA Ops:
  6.5 309.6 %copy-start = (bf16[1280,1280]{1,0:T(8,128)(2,1)S(1)}, bf16[1280,1280]{1,0:T(8,128)(2,1)}, u32[]{:S(2)}) copy-start(bf16[1280,1280]{1,0:T(8,128)(2,1)} %param.9) | copy-start | bytes 9830404
  6.5 24.2 %all-gather.6.cloned.1.call-start = ((), (), s32[]{:S(2)}) async-start(), calls=%async_computation.4 | async-start | bytes 1843200 | tf_op jit(solution)/shard_map/all_gather | solution.py:65
  7.3 83.6 %all-gather.4.cloned.1.call-start = ((), (), s32[]{:S(2)}) async-start(), calls=%async_computation.3 | async-start | bytes 3317760 | tf_op jit(solution)/shard_map/all_gather | solution.py:70
  8.0 141.7 %all-gather.8.cloned.1.call-start = ((), (), s32[]{:S(2)}) async-start(), calls=%async_computation.5 | async-start | bytes 3317760 | tf_op jit(solution)/shard_map/all_gather | solution.py:71
  173.6 10.4 %copy-start.1 = (f32[20,576]{1,0:T(8,128)S(1)}, f32[20,576]{1,0:T(8,128)}, u32[]{:S(2)}) copy-start(f32[20,576]{1,0:T(8,128)} %get-tuple-element.262) | copy-start | bytes 138244 | tf_op jit(solution)/shard_map/while
  184.0 20.7 %copy-start.2 = (f32[20,576]{1,0:T(8,128)}, f32[20,576]{1,0:T(8,128)S(1)}, u32[]{:S(2)}) copy-start(f32[20,576]{1,0:T(8,128)S(1)} %fusion.29) | copy-start | bytes 138244 | tf_op jit(solution)/shard_map/while
  226.7 10.4 %copy-start.1 = (f32[20,576]{1,0:T(8,128)S(1)}, f32[20,576]{1,0:T(8,128)}, u32[]{:S(2)}) copy-start(f32[20,576]{1,0:T(8,128)} %get-tuple-element.262) | copy-start | bytes 138244 | tf_op jit(solution)/shard_map/while
  237.2 20.7 %copy-start.2 = (f32[20,576]{1,0:T(8,128)}, f32[20,576]{1,0:T(8,128)S(1)}, u32[]{:S(2)}) copy-start(f32[20,576]{1,0:T(8,128)S(1)} %fusion.29) | copy-start | bytes 138244 | tf_op jit(solution)/shard_map/while
  258.8 7.4 %all-to-all-start.1 = ((f32[4,1,2880]{2,1,0:T(1,128)}), f32[4,1,2880]{2,1,0:T(1,128)S(1)}, u32[]{:S(2)}, u32[]{:S(2)}) async-start(f32[4,1,2880]{2,1,0:T(1,128)} %reshape.60), calls=%async_computation.1 | async-start | bytes 94208 | tf_op jit(solution)/shard_map/all_to_all | solution.py:79
  266.2 7.3 %all-to-all-start.2 = ((f32[4,1,2880]{2,1,0:T(1,128)}), f32[4,1,2880]{2,1,0:T(1,128)S(1)}, u32[]{:S(2)}, u32[]{:S(2)}) async-start(f32[4,1,2880]{2,1,0:T(1,128)} %reshape.62), calls=%async_computation.2 | async-start | bytes 94208 | tf_op jit(solution)/shard_map/all_to_all | solution.py:80
  273.5 39.5 %all-to-all-start = ((f32[4,144,1280]{2,1,0:T(8,128)}), f32[4,144,1280]{2,1,0:T(8,128)}, u32[]{:S(2)}, u32[]{:S(2)}) async-start(f32[4,144,1280]{2,1,0:T(8,128)} %bitcast.72), calls=%async_computation | async-start | bytes 5898240 | tf_op jit(solution)/shard_map/all_to_all | solution.py:78
  313.0 3.2 copy-start.3
Sparse Core Ops, SparseCore 0:
  8.9 21.7 all-gather.5
  32.9 57.9 all-gather.3
  93.1 56.5 all-gather.7
where the time goes:
time: 325 us; the launch traced here: 324 us
  waiting for transfers between devices  157 us (48%)
  matrix products  68.7 us (21%)
  local copies, waits for them, and re-layouts  47.4 us (15%)
  other arithmetic  26.3 us (8%)
  between operations  13.2 us (4%)
  starting transfers between devices  11.4 us (4%)
    all_gather x1, waiting for transfers between devices, per_device(): lax.all_gather(value, 'blk', axis=0, tiled=True)  58.8 us
    all_gather x1, waiting for transfers between devices, per_device(): lax.all_gather(key, 'blk', axis=0, tiled=True)  57.5 us
    dot_general x2, matrix products, update(): jnp.einsum('hqk,khd->qhd', expo.astype(jnp.bfloat16), value_block, prefer...  36 us
    dot_general x2, matrix products, update(): jnp.einsum('qhd,khd->hqk', queries, key_block, preferred_element_type=jnp...  31.3 us
    all_gather x1, waiting for transfers between devices, per_device(): gathered = lax.all_gather(query, 'node', axis=0, tiled=True)  22 us
    reduce_sum x2, other arithmetic, update(): total = total * factor + jnp.sum(expo, axis=2)  20.8 us
    all_to_all x1, waiting for transfers between devices, per_device(): lax.all_to_all(acc_parts, 'node', split_axis=0, concat_axis=0, tiled=True)  14 us
    dynamic_slice x4, local copies, waits for them, and re-layouts, update(): lax.dynamic_slice_in_dim(values_piece, turn * size, size, 0)  12.7 us
  transfers between devices with their start and end apart: 6, of which 6 were waited for; matrix products, arithmetic and copies ran while one was open for 9% of the time, Pallas kernels for 0%

commit v1 on v0

--- a/solution.py
+++ b/solution.py
@@ -62,7 +62,12 @@
 def per_device(query, key, value, out_weight):
     rows, features = query.shape
     heads = features // HD
-    gathered = lax.all_gather(query, "node", axis=0, tiled=True)
+    ring = [query]
+    for hop in range(3):
+        ring.append(lax.ppermute(ring[-1], "node", [(dev, (dev + 1) % 4) for dev in range(4)]))
+    gathered = jnp.roll(
+        jnp.concatenate(ring[::-1], axis=0), (lax.axis_index("node") + 1) * ring[0].shape[0], axis=0
+    )
     count = gathered.shape[0]
     q_three = gathered.reshape(count, heads, HD)
     peak, total, accum = attend(

time: 325 us -> 305 us (0.938)
  waiting for transfers between devices: 157 us -> 128 us
  local copies, waits for them, and re-layouts: 47.4 us -> 55.1 us
    all_gather x1, waiting for transfers between devices: 57.5 us -> 29.7 us  [per_device(): lax.all_gather(key, 'blk', axis=0, tiled=True)]
    all_gather x1 -> x0, waiting for transfers between devices: 22 us -> none  [per_device(): gathered = lax.all_gather(query, 'node', axis=0, tiled=True)]
    ppermute x0 -> x3, waiting for transfers between devices: none -> 21.5 us  [per_device(): lax.ppermute(ring[-1], 'node', [(dev, (dev + 1) % 4) for dev in range(4)])]
    unnamed x8 -> x21, local copies, waits for them, and re-layouts: 1.72 us -> 7.86 us
    dynamic_slice x0 -> x2, local copies, waits for them, and re-layouts: none -> 4.15 us  [per_device(): jnp.roll(jnp.concatenate(ring[::-1], axis=0), (lax.axis_index('node') + 1...]
  transfers between devices with their start and end apart: 6 -> 8, of which waited for: 6 -> 8; matrix products, arithmetic and copies ran while one was open for 9% -> 12% of each run, Pallas kernels for 0% -> 0%
where the time goes in v1:
time: 305 us; the launch traced here: 304 us
  waiting for transfers between devices  128 us (42%)
  matrix products  68.7 us (23%)
  local copies, waits for them, and re-layouts  55.1 us (18%)
  other arithmetic  26.3 us (9%)
  between operations  13.6 us (4%)
  starting transfers between devices  12 us (4%)
    all_gather x1, waiting for transfers between devices, per_device(): lax.all_gather(value, 'blk', axis=0, tiled=True)  58.8 us
    dot_general x2, matrix products, update(): jnp.einsum('hqk,khd->qhd', expo.astype(jnp.bfloat16), value_block, prefer...  36 us
    dot_general x2, matrix products, update(): jnp.einsum('qhd,khd->hqk', queries, key_block, preferred_element_type=jnp...  31.3 us
    all_gather x1, waiting for transfers between devices, per_device(): lax.all_gather(key, 'blk', axis=0, tiled=True)  29.7 us
    ppermute x3, waiting for transfers between devices, per_device(): lax.ppermute(ring[-1], 'node', [(dev, (dev + 1) % 4) for dev in range(4)])  21.5 us
    reduce_sum x2, other arithmetic, update(): total = total * factor + jnp.sum(expo, axis=2)  20.8 us
    all_to_all x1, waiting for transfers between devices, per_device(): lax.all_to_all(acc_parts, 'node', split_axis=0, concat_axis=0, tiled=True)  14 us
    dynamic_slice x4, local copies, waits for them, and re-layouts, update(): lax.dynamic_slice_in_dim(values_piece, turn * size, size, 0)  12.7 us
  transfers between devices with their start and end apart: 8, of which 8 were waited for; matrix products, arithmetic and copies ran while one was open for 12% of the time, Pallas kernels for 0%

profile of v1, /device:TPU:0, one launch (start us, length us, event | category | flops | bytes accessed | tf_op | source)
XLA Modules:
  0.0 303.7 jit_solution(9686499163801225804)
XLA Ops:
  6.5 0.7 all-gather.3.cloned.1.call-update
  7.3 0.7 all-gather.5.cloned.1.call-update
  8.6 7.3 %collective-permute-done = bf16[144,1280]{1,0:T(8,128)(2,1)S(1)} collective-permute-done((bf16[144,1280]{1,0:T(8,128)(2,1)}, bf16[144,1280]{1,0:T(8,128)(2,1)S(1)}, u32[]{:S(2)}, u32[]{:S(2)}) %collective-permute-start) | collective-permute-done | bytes 368672 | tf_op jit(solution)/shard_map/ppermute | solution.py:67
  15.9 7.0 %collective-permute-done.1 = bf16[144,1280]{1,0:T(8,128)(2,1)} collective-permute-done((bf16[144,1280]{1,0:T(8,128)(2,1)S(1)}, bf16[144,1280]{1,0:T(8,128)(2,1)}, u32[]{:S(2)}, u32[]{:S(2)}) %collective-permute-start.1) | collective-permute-done | bytes 368672 | tf_op jit(solution)/shard_map/ppermute | solution.py:67
  23.0 7.2 %collective-permute-done.2 = bf16[144,1280]{1,0:T(8,128)(2,1)} collective-permute-done((bf16[144,1280]{1,0:T(8,128)(2,1)}, bf16[144,1280]{1,0:T(8,128)(2,1)}, u32[]{:S(2)}, u32[]{:S(2)}) %collective-permute-start.2) | collective-permute-done | bytes 368672 | tf_op jit(solution)/shard_map/ppermute | solution.py:67
  30.2 1.0 constant_dynamic-update-slice_fusion.7
  31.2 1.0 constant_dynamic-update-slice_fusion.6
  32.2 1.0 constant_dynamic-update-slice_fusion.5
  33.2 1.0 constant_dynamic-update-slice_fusion.4
  34.3 1.0 constant_dynamic-update-slice_fusion.3
  35.3 1.0 constant_dynamic-update-slice_fusion.2
  36.4 1.5 constant_dynamic-slice_fusion.2
  37.9 2.7 copy.30
  40.5 29.7 %all-gather.3.cloned.1.call-done = bf16[1152,1280]{1,0:T(8,128)(2,1)} async-done(((bf16[144,1280]{1,0:T(8,128)(2,1)}), bf16[1152,1280]{1,0:T(8,128)(2,1)}) %all-gather.3.cloned.1.call-update) | async-done | bytes 2949136 | tf_op jit(solution)/shard_map/all_gather | solution.py:75
  70.2 58.8 %all-gather.5.cloned.1.call-done = bf16[1152,1280]{1,0:T(8,128)(2,1)} async-done(((bf16[144,1280]{1,0:T(8,128)(2,1)}), bf16[1152,1280]{1,0:T(8,128)(2,1)}) %all-gather.5.cloned.1.call-update) | async-done | bytes 2949136 | tf_op jit(solution)/shard_map/all_gather | solution.py:76
  129.0 1.9 broadcast_in_dim.20
  130.9 106.4 %while.18 = (s32[]{:T(128)}, f32[20,576]{1,0:T(8,128)S(1)}, f32[20,576]{1,0:T(8,128)}, f32[576,1280]{0,1:T(8,128)}, bf16[1152,1280]{1,0:T(8,128)(2,1)}, /*index=...) while((s32[]{:T(128)}, f32[20,576]{1,0:T(8,128)S(1)}, ...), condition=%wide.region_3.4_spmd.clone, body=%wide.region_0.3_spmd.clone.sunk | while | flops 1753320960 | bytes 102850792 | solution.py:51
  130.9 3.7 %constant_dynamic-slice_fusion.4 = (bf16[576,1280]{1,0:T(8,128)(2,1)}, bf16[576,1280]{1,0:T(8,128)(2,1)}) fusion(bf16[1152,1280]{1,0:T(8,128)(2,1)} %get-tuple-element.277, s32[]{:T(128)S(6)} %select_n.25, bf16[1152,1280]{1,0:T(8,128)(2,1)} %get-tuple-element.275), kind=kLoop, calls=%fused_computation.14.clone.1 | loop fusion | bytes 5898244 | tf_op jit(solution)/shard_map/while/body/eval_jaxpr/dynamic_slice | solution.py:29
  134.6 2.7 copy.49
  137.2 15.7 %bitcast_reduce_fusion.3 = (f32[20,576]{1,0:T(8,128)S(1)}, f32[20,576,576]{2,1,0:T(8,128)}) fusion(bf16[576,20,64]{0,2,1:T(8,128)(2,1)} %bitcast.67, bf16[576,20,64]{0,2,1:T(8,128)(2,1)} %get-tuple-element.276), kind=kOutput, calls=%fused_computation.1.clone.1 | convolution fusion | flops 862606080 | bytes 29537280 | tf_op jit(solution)/shard_map/while/body/eval_jaxpr/qhd,khd->hqk/dot_general | solution.py:33
  152.9 10.4 %fusion.28 = f32[20,576]{1,0:T(8,128)S(1)} fusion(f32[20,576,576]{2,1,0:T(8,128)} %get-tuple-element.246, f32[20,576]{1,0:T(8,128)S(1)} %get-tuple-element.272), kind=kLoop, calls=%fused_computation.4.clone.1 | loop fusion | flops 19895040 | bytes 26634240 | tf_op jit(solution)/shard_map/while/body/eval_jaxpr/reduce_sum | solution.py:39
  163.4 2.7 copy.50
  166.1 18.0 %bitcast_add_fusion.2 = f32[576,20,64]{0,2,1:T(8,128)} fusion(f32[576,20,64]{0,2,1:T(8,128)} %bitcast.70, bf16[576,20,64]{0,2,1:T(8,128)(2,1)} %bitcast.69, f32[20,576,576]{2,1,0:T(8,128)} %get-tuple-element.246, f32[20,576]{1,0:T(8,128)S(1)} %get-tuple-element.272, f32[576,20]{0,1:T(8,128)S(1)} %get-tuple-element.248), kind=kOutput, calls=%fused_computation.8.clone.1 | convolution fusion | flops 870727680 | bytes 34007040 | tf_op jit(solution)/shard_map/while/body/eval_jaxpr/hqk,khd->qhd/dot_general | solution.py:40
  184.1 3.7 %constant_dynamic-slice_fusion.4 = (bf16[576,1280]{1,0:T(8,128)(2,1)}, bf16[576,1280]{1,0:T(8,128)(2,1)}) fusion(bf16[1152,1280]{1,0:T(8,128)(2,1)} %get-tuple-element.277, s32[]{:T(128)S(6)} %select_n.25, bf16[1152,1280]{1,0:T(8,128)(2,1)} %get-tuple-element.275), kind=kLoop, calls=%fused_computation.14.clone.1 | loop fusion | bytes 5898244 | tf_op jit(solution)/shard_map/while/body/eval_jaxpr/dynamic_slice | solution.py:29
  187.7 2.7 copy.49
  190.4 15.7 %bitcast_reduce_fusion.3 = (f32[20,576]{1,0:T(8,128)S(1)}, f32[20,576,576]{2,1,0:T(8,128)}) fusion(bf16[576,20,64]{0,2,1:T(8,128)(2,1)} %bitcast.67, bf16[576,20,64]{0,2,1:T(8,128)(2,1)} %get-tuple-element.276), kind=kOutput, calls=%fused_computation.1.clone.1 | convolution fusion | flops 862606080 | bytes 29537280 | tf_op jit(solution)/shard_map/while/body/eval_jaxpr/qhd,khd->hqk/dot_general | solution.py:33
  206.1 10.4 %fusion.28 = f32[20,576]{1,0:T(8,128)S(1)} fusion(f32[20,576,576]{2,1,0:T(8,128)} %get-tuple-element.246, f32[20,576]{1,0:T(8,128)S(1)} %get-tuple-element.272), kind=kLoop, calls=%fused_computation.4.clone.1 | loop fusion | flops 19895040 | bytes 26634240 | tf_op jit(solution)/shard_map/while/body/eval_jaxpr/reduce_sum | solution.py:39
  216.6 2.7 copy.50
  219.3 18.0 %bitcast_add_fusion.2 = f32[576,20,64]{0,2,1:T(8,128)} fusion(f32[576,20,64]{0,2,1:T(8,128)} %bitcast.70, bf16[576,20,64]{0,2,1:T(8,128)(2,1)} %bitcast.69, f32[20,576,576]{2,1,0:T(8,128)} %get-tuple-element.246, f32[20,576]{1,0:T(8,128)S(1)} %get-tuple-element.272, f32[576,20]{0,1:T(8,128)S(1)} %get-tuple-element.248), kind=kOutput, calls=%fused_computation.8.clone.1 | convolution fusion | flops 870727680 | bytes 34007040 | tf_op jit(solution)/shard_map/while/body/eval_jaxpr/hqk,khd->qhd/dot_general | solution.py:40
  237.4 0.8 reshape.60
  238.2 3.3 %all-to-all-start.1 = ((f32[4,1,2880]{2,1,0:T(1,128)}), f32[4,1,2880]{2,1,0:T(1,128)S(1)}, u32[]{:S(2)}, u32[]{:S(2)}) async-start(f32[4,1,2880]{2,1,0:T(1,128)} %reshape.60), calls=%async_computation.1 | async-start | bytes 94208 | tf_op jit(solution)/shard_map/all_to_all | solution.py:84
  241.4 0.9 reshape.55
  242.4 0.8 reshape.62
  243.1 2.3 all-to-all-done.1
  245.4 3.5 %all-to-all-start.2 = ((f32[4,1,2880]{2,1,0:T(1,128)}), f32[4,1,2880]{2,1,0:T(1,128)S(1)}, u32[]{:S(2)}, u32[]{:S(2)}) async-start(f32[4,1,2880]{2,1,0:T(1,128)} %reshape.62), calls=%async_computation.2 | async-start | bytes 94208 | tf_op jit(solution)/shard_map/all_to_all | solution.py:85
  248.9 3.6 %copy.33 = f32[576,1280]{1,0:T(8,128)} copy(f32[576,1280]{0,1:T(8,128)} %get-tuple-element.131) | data formatting | bytes 5898240 | tf_op jit(solution)/shard_map/while | solution.py:51
  252.7 4.6 %all-to-all-start = ((f32[4,144,1280]{2,1,0:T(8,128)}), f32[4,144,1280]{2,1,0:T(8,128)}, u32[]{:S(2)}, u32[]{:S(2)}) async-start(f32[4,144,1280]{2,1,0:T(8,128)} %bitcast.72), calls=%async_computation | async-start | bytes 5898240 | tf_op jit(solution)/shard_map/all_to_all | solution.py:83
  257.8 0.8 reduce.1
  258.7 0.8 reduce.2
  259.6 0.7 multiply_reduce_fusion.1
  260.3 1.8 copy.35
  262.1 5.3 %mul.63 = f32[4,144,20,64]{3,2,1,0:T(8,128)} broadcast(f32[4,144,20]{2,1,0:T(8,128)} %copy.35), dimensions={0,1,2} | broadcast | bytes 2995200 | tf_op jit(solution)/shard_map/mul | solution.py:91
  267.4 6.4 %mul.64 = f32[4,144,1280]{2,1,0:T(8,128)} reshape(f32[4,144,20,64]{3,2,1,0:T(8,128)} %mul.63) | data formatting | bytes 5898240 | tf_op jit(solution)/shard_map/mul | solution.py:91
  273.8 1.8 div.11
  275.6 2.6 div.12
  278.2 14.0 %all-to-all-done = f32[4,144,1280]{2,1,0:T(8,128)} async-done(((f32[4,144,1280]{2,1,0:T(8,128)}), f32[4,144,1280]{2,1,0:T(8,128)}, u32[]{:S(2)}, u32[]{:S(2)}) %all-to-all-start) | async-done | bytes 2949152 | tf_op jit(solution)/shard_map/all_to_all | solution.py:83
  292.2 3.2 %multiply_reduce_fusion = f32[144,1280]{1,0:T(8,128)S(1)} fusion(f32[4,144,1280]{2,1,0:T(8,128)} %all-to-all-done, f32[4,144,1280]{2,1,0:T(8,128)} %mul.64), kind=kLoop, calls=%fused_computation.17 | loop fusion | flops 1290240 | bytes 6635520 | tf_op jit(solution)/shard_map/reduce_sum | solution.py:91
  295.4 1.4 convolution_convert_fusion
  (42 shorter events, 2.1 us)
Async XLA Ops:
  6.5 288.9 %copy-start = (bf16[1280,1280]{1,0:T(8,128)(2,1)S(1)}, bf16[1280,1280]{1,0:T(8,128)(2,1)}, u32[]{:S(2)}) copy-start(bf16[1280,1280]{1,0:T(8,128)(2,1)} %param.9) | copy-start | bytes 9830404
  6.5 63.7 %all-gather.3.cloned.1.call-start = ((), (), s32[]{:S(2)}) async-start(), calls=%async_computation.3 | async-start | bytes 3317760 | tf_op jit(solution)/shard_map/all_gather | solution.py:75
  7.3 121.7 %all-gather.5.cloned.1.call-start = ((), (), s32[]{:S(2)}) async-start(), calls=%async_computation.4 | async-start | bytes 3317760 | tf_op jit(solution)/shard_map/all_gather | solution.py:76
  8.0 7.9 %collective-permute-start = (bf16[144,1280]{1,0:T(8,128)(2,1)}, bf16[144,1280]{1,0:T(8,128)(2,1)S(1)}, u32[]{:S(2)}, u32[]{:S(2)}) collective-permute-start(bf16[144,1280]{1,0:T(8,128)(2,1)} %param.6), channel_id=1, source_target_pairs={{0,1},{1,2},{2,3},{3,0},{4,5},{5,6},{6,7},{7,4},{8,9},{9,10},{10,1... | collective-permute-start | bytes 1105928 | tf_op jit(solution)/shard_map/ppermute | solution.py:67
  15.9 7.0 %copy-start.4 = (bf16[144,1280]{1,0:T(8,128)(2,1)}, bf16[144,1280]{1,0:T(8,128)(2,1)S(1)}, u32[]{:S(2)}) copy-start(bf16[144,1280]{1,0:T(8,128)(2,1)S(1)} %collective-permute-done) | copy-start | bytes 1105924
  15.9 7.0 %collective-permute-start.1 = (bf16[144,1280]{1,0:T(8,128)(2,1)S(1)}, bf16[144,1280]{1,0:T(8,128)(2,1)}, u32[]{:S(2)}, u32[]{:S(2)}) collective-permute-start(bf16[144,1280]{1,0:T(8,128)(2,1)S(1)} %collective-permute-done), channel_id=1, source_target_pairs={{0,1},{1,2},{2,3},{3,0},{4,5},{5,6},{6,7},{7,4},{8,9},{9,10},{10,1... | collective-permute-start | bytes 1105928 | tf_op jit(solution)/shard_map/ppermute | solution.py:67
  22.9 7.3 %collective-permute-start.2 = (bf16[144,1280]{1,0:T(8,128)(2,1)}, bf16[144,1280]{1,0:T(8,128)(2,1)}, u32[]{:S(2)}, u32[]{:S(2)}) collective-permute-start(bf16[144,1280]{1,0:T(8,128)(2,1)} %collective-permute-done.1), channel_id=1, source_target_pairs={{0,1},{1,2},{2,3},{3,0},{4,5},{5,6},{6,7},{7,4},{8,9},{9,10},{10,1... | collective-permute-start | bytes 1105928 | tf_op jit(solution)/shard_map/ppermute | solution.py:67
  23.0 13.3 %copy-start.5 = (bf16[144,1280]{1,0:T(8,128)(2,1)S(1)}, bf16[144,1280]{1,0:T(8,128)(2,1)}, u32[]{:S(2)}) copy-start(bf16[144,1280]{1,0:T(8,128)(2,1)} %copy-done.4) | copy-start | bytes 1105924
  23.0 13.4 %copy-start.3 = (bf16[144,1280]{1,0:T(8,128)(2,1)S(1)}, bf16[144,1280]{1,0:T(8,128)(2,1)}, u32[]{:S(2)}) copy-start(bf16[144,1280]{1,0:T(8,128)(2,1)} %param.6) | copy-start | bytes 1105924
  152.9 10.4 %copy-start.1 = (f32[20,576]{1,0:T(8,128)S(1)}, f32[20,576]{1,0:T(8,128)}, u32[]{:S(2)}) copy-start(f32[20,576]{1,0:T(8,128)} %get-tuple-element.262) | copy-start | bytes 138244 | tf_op jit(solution)/shard_map/while
  163.4 20.7 %copy-start.2 = (f32[20,576]{1,0:T(8,128)}, f32[20,576]{1,0:T(8,128)S(1)}, u32[]{:S(2)}) copy-start(f32[20,576]{1,0:T(8,128)S(1)} %fusion.29) | copy-start | bytes 138244 | tf_op jit(solution)/shard_map/while
  206.1 10.4 %copy-start.1 = (f32[20,576]{1,0:T(8,128)S(1)}, f32[20,576]{1,0:T(8,128)}, u32[]{:S(2)}) copy-start(f32[20,576]{1,0:T(8,128)} %get-tuple-element.262) | copy-start | bytes 138244 | tf_op jit(solution)/shard_map/while
  216.6 20.7 %copy-start.2 = (f32[20,576]{1,0:T(8,128)}, f32[20,576]{1,0:T(8,128)S(1)}, u32[]{:S(2)}) copy-start(f32[20,576]{1,0:T(8,128)S(1)} %fusion.29) | copy-start | bytes 138244 | tf_op jit(solution)/shard_map/while
  238.2 7.3 %all-to-all-start.1 = ((f32[4,1,2880]{2,1,0:T(1,128)}), f32[4,1,2880]{2,1,0:T(1,128)S(1)}, u32[]{:S(2)}, u32[]{:S(2)}) async-start(f32[4,1,2880]{2,1,0:T(1,128)} %reshape.60), calls=%async_computation.1 | async-start | bytes 94208 | tf_op jit(solution)/shard_map/all_to_all | solution.py:84
  245.4 7.3 %all-to-all-start.2 = ((f32[4,1,2880]{2,1,0:T(1,128)}), f32[4,1,2880]{2,1,0:T(1,128)S(1)}, u32[]{:S(2)}, u32[]{:S(2)}) async-start(f32[4,1,2880]{2,1,0:T(1,128)} %reshape.62), calls=%async_computation.2 | async-start | bytes 94208 | tf_op jit(solution)/shard_map/all_to_all | solution.py:85
  252.7 39.5 %all-to-all-start = ((f32[4,144,1280]{2,1,0:T(8,128)}), f32[4,144,1280]{2,1,0:T(8,128)}, u32[]{:S(2)}, u32[]{:S(2)}) async-start(f32[4,144,1280]{2,1,0:T(8,128)} %bitcast.72), calls=%async_computation | async-start | bytes 5898240 | tf_op jit(solution)/shard_map/all_to_all | solution.py:83
  292.2 3.2 %copy-start.6 = (f32[144,1280]{1,0:T(8,128)S(1)}, f32[144,1280]{1,0:T(8,128)}, u32[]{:S(2)}) copy-start(f32[144,1280]{1,0:T(8,128)} %div.12) | copy-start | bytes 2211844
Sparse Core Ops, SparseCore 0:
  9.5 60.6 all-gather.2
  72.4 56.5 all-gather.4
